TPU v7x, 32 devices: a whole 2x2x4 slice. The times are simulated.
32 devices in a mesh: dp: 8 (over y, x, core), fsdp: 4 (over z).
Axes of the slice: x: 2, y: 2, z: 4, core: 2. Of those that a mesh axis runs over, the one named last changes fastest.
Arguments:
- grads: float32 [32, 96, 128], P(('dp', 'fsdp')), may hold values from -0.6 to 0.6
- last_peak: float32 [96], replicated, may hold values from 0.05 to 0.8
- master: float32 [96, 128], P(('dp', 'fsdp')), may hold values from -6 to 6
- moment1: float32 [96, 128], P(('dp', 'fsdp')), may hold values from -6 to 6
- moment2: float32 [96, 128], P(('dp', 'fsdp')), may hold values from 0.25 to 8
Outputs:
- new_master: float32 [96, 128], P(('dp', 'fsdp'))
- new_moment1: float32 [96, 128], P(('dp', 'fsdp'))
- new_moment2: float32 [96, 128], P(('dp', 'fsdp'))
- weights: bfloat16 [96, 128], replicated
- block_peak: float32 [96], replicated
All inputs are finite; a program needn't handle non-finite values.
Results may differ from a plain program's by a relative error of at most 0.0035.
Values may be sent and summed in bfloat16 or wider, within the bound.
A program may use at most 64 MiB of HBM per device.

v0:
```python
import functools

import jax
import jax.numpy as jnp
from jax import lax
from jax.experimental import pallas as pl
from jax.experimental.pallas import tpu as pltpu
from jax.sharding import PartitionSpec as P

STEP_COUNT = 10


code_limit = 448.0
peak_floor = 0.05
beta_one = 0.9
beta_two = 0.95
learn_rate = 0.05
decay_rate = 0.1
epsilon = 1e-08
AXES = ("dp", "fsdp")
UNROLL_MOST = 64
ROOT_BYTES = 8 * 2**20


def adamw(gradient, master, moment1, moment2):
    first = beta_one * moment1 + (1.0 - beta_one) * gradient
    second = beta_two * moment2 + (1.0 - beta_two) * gradient * gradient
    corrected_one = first * (1.0 / (1.0 - beta_one**STEP_COUNT))
    corrected_two = second * (1.0 / (1.0 - beta_two**STEP_COUNT))
    updated = master - learn_rate * (
        corrected_one / (jnp.sqrt(corrected_two) + epsilon) + decay_rate * master
    )
    return (updated, first, second)


def layout(sizes, blocks, width):
    dp, fsdp = sizes
    pair = 2 if dp % 2 == 0 else 1
    above = min(1, fsdp - 1)
    proxies = [(pair * q + pair - 1, above) for q in range(dp // pair)]
    collector = (min(3, dp - 1), 0)
    mates = [(k, 0) for k in range(pair)]
    fits = 2 * dp * fsdp * blocks * width <= ROOT_BYTES
    if above == 0 or pair == 1 or dp < 4 * pair or dp % (2 * pair) or not fits:
        mates = []
    return pair, proxies, collector, mates


def gathering(sizes):
    dp, fsdp = sizes
    half = dp // 4
    places = [(2 * g + 1 if g == half else 2 * (g - half) + 1, 0) for g in range(half, 2 * half)]
    return min(2, fsdp - 1), half, places


def kernel(
    sizes,
    grads_hbm,
    last_peak_hbm,
    master_hbm,
    moment1_hbm,
    moment2_hbm,
    updated_ref,
    first_ref,
    second_ref,
    weights_ref,
    peak_ref,
    grads,
    last_peak,
    state,
    codes,
    message,
    received,
    states,
    column,
    gradient_out,
    gradient_in,
    peak_message,
    peak_received,
    peak_out,
    peak_in,
    in_sems,
    recv_sems,
    send_sem,
    state_send,
    state_recv,
    grad_send,
    grad_recv,
    out_send,
    out_recv,
    peak_send,
    peak_recv,
    top_send,
    top_recv,
    *root_refs,
):
    dp, fsdp = sizes
    n = dp * fsdp
    blocks, width = message.shape
    pair, proxies, collector, mates = layout(sizes, blocks, width)
    count = len(proxies)
    hubs = proxies + [collector] + mates
    owned = blocks // n
    part = blocks // count
    lines = peak_out.shape[0]
    mine, level = lax.axis_index("dp"), lax.axis_index("fsdp")
    me = mine * fsdp + level
    slot = level * dp + mine
    group = lax.div(mine, pair)
    seat = lax.rem(mine, pair) * fsdp + level

    def at_place(where):
        return jnp.logical_and(mine == where[0], level == where[1])

    def any_of(flags):
        return functools.reduce(jnp.logical_or, flags, jnp.bool_(False))

    def unless(flag):
        return pl.when(jnp.logical_not(flag))

    is_proxy = any_of([at_place(where) for where in proxies])
    is_collector = at_place(collector)
    is_mate = any_of([at_place(where) for where in mates])
    is_hub = any_of([is_proxy, is_collector, is_mate])
    if mates:
        root = mates[-1]
        is_root = at_place(root)
        skip, kept = part, blocks - part
        rest = message.at[pl.ds(skip, kept)]
        is_kept = me * owned >= skip
        mate = mates[0]
        is_first = at_place(mate)
        near_levels, half, combiners = gathering(sizes)
        nears = []
        for at in range(half):
            chip = (half + at) * pair
            nears.append([(k, f) for f in range(near_levels) for k in range(chip, chip + pair)])
        in_nears = [jnp.logical_and(level < near_levels, group == half + at) for at in range(half)]
        is_near = any_of(in_nears)
        idle = [where for where, near in zip(combiners, nears) if where in near]
        is_idle = any_of([at_place(where) for where in idle])
        (
            all_received,
            all_states,
            all_column,
            near_received,
            partial_out,
            partial_in,
            all_recv,
            all_send,
            all_state_send,
            all_state_recv,
            near_recv,
            partial_send,
            partial_recv,
            early_out,
            early_in,
            early_send,
            early_recv,
            far_send,
            mate_state_send,
        ) = root_refs

    def remote(source, target, send, recv, where):
        return pltpu.make_async_remote_copy(
            src_ref=source,
            dst_ref=target,
            send_sem=send,
            recv_sem=recv,
            device_id=where,
            device_id_type=pl.DeviceIdType.MESH,
        )

    def drain(ref, sem):
        pltpu.make_async_copy(ref, ref, sem).wait()

    def others(step, skipped=()):
        if n <= UNROLL_MOST:
            near = [(k, f) for f in range(fsdp) for k in range(pair)]
            far = [(k, f) for f in range(fsdp) for k in range(pair, dp)]
            for where in near + far:
                if where not in skipped:
                    unless(at_place(where))(functools.partial(step, where))
        else:

            def turn(k, carry):
                other = lax.rem(me + k, n)
                step((lax.div(other, fsdp), lax.rem(other, fsdp)))
                return carry

            lax.fori_loop(1, n, turn, 0)

    loads = [
        pltpu.make_async_copy(source, target, in_sems.at[at])
        for at, (source, target) in enumerate(
            (
                (last_peak_hbm, last_peak),
                (grads_hbm.at[:, pl.ds(0, part)], grads.at[:, pl.ds(0, part)]),
                (grads_hbm.at[:, pl.ds(part, blocks - part)], grads.at[:, pl.ds(part, blocks - part)]),
                (master_hbm, state.at[0]),
                (moment1_hbm, state.at[1]),
                (moment2_hbm, state.at[2]),
            )
        )
    ]
    for load in loads:
        load.start()
    barrier = pltpu.get_barrier_semaphore()

    def greet(where):
        pl.semaphore_signal(
            barrier, inc=1, device_id=where, device_id_type=pl.DeviceIdType.MESH
        )

    @pl.when(is_hub)
    def _():
        others(greet)

    if mates:

        for combiner, near in zip(combiners, nears):
            if combiner not in hubs:

                @pl.when(at_place(combiner))
                def _():
                    for where in near:
                        if where != combiner:
                            greet(where)

    loads[0].wait()
    floored = jnp.maximum(last_peak[...], peak_floor)
    inverse = code_limit / floored
    scale = floored / code_limit
    row = lax.broadcasted_iota(jnp.int32, (blocks, blocks), 0)
    lane = lax.broadcasted_iota(jnp.int32, (blocks, blocks), 1)
    diagonal = row == lane
    inverse_column = jnp.sum(jnp.where(diagonal, inverse, 0.0), axis=1, keepdims=True)
    def encode(first, rows):
        scaled = grads[0, pl.ds(first, rows), :] * inverse_column[first : first + rows]
        message[pl.ds(first, rows), :] = jnp.clip(scaled, -code_limit, code_limit).astype(jnp.bfloat16)

    loads[1].wait()
    encode(0, part)

    if mates:
        greeted_more = any_of(
            [flag for flag, combiner in zip(in_nears, combiners) if combiner not in hubs]
        )
        greeted_more = jnp.logical_and(greeted_more, jnp.logical_not(is_idle))
        for flag, more in ((greeted_more, 1), (jnp.logical_not(greeted_more), 0)):

            @pl.when(jnp.logical_and(flag, is_hub))
            def _():
                pl.semaphore_wait(barrier, len(hubs) - 1 + more)

            @pl.when(jnp.logical_and(flag, jnp.logical_not(is_hub)))
            def _():
                pl.semaphore_wait(barrier, len(hubs) + more)

    else:

        @pl.when(is_hub)
        def _():
            pl.semaphore_wait(barrier, len(hubs) - 1)

        @unless(is_hub)
        def _():
            pl.semaphore_wait(barrier, len(hubs))

    last = fsdp - 1
    lateness = lax.div(level, max(last, 1))

    def send_part(q, where):
        @unless(at_place(where))
        def _():
            source = message.at[pl.ds(q * part, part)]
            remote(source, received.at[slot], send_sem, recv_sems.at[level], where).start()

    if mates:

        @pl.when(level == last)
        def _():
            source = message.at[pl.ds(0, part)]
            remote(source, received.at[slot], far_send, recv_sems.at[level], mate).start()

        @unless(level == last)
        def _():
            send_part(0, proxies[0])

    else:
        send_part(0, proxies[0])
    loads[2].wait()
    encode(part, blocks - part)
    values = grads[0]

    if mates:

        @unless(jnp.logical_or(is_root, is_near))
        def _():
            remote(rest, all_received.at[slot], all_send, all_recv.at[level], root).start()

        for at, combiner in enumerate(combiners):

            @pl.when(jnp.logical_and(in_nears[at], jnp.logical_not(at_place(combiner))))
            def _():
                target = near_received.at[level * pair + mine - (half + at) * pair]
                remote(rest, target, all_send, near_recv, combiner).start()

        @pl.when(level == last)
        def _():
            send_part(0, proxies[0])

    for load in loads[3:]:
        load.wait()
    if mates:

        @pl.when(is_kept)
        def _():
            target = all_states.at[me - skip // owned]
            remote(state, target, all_state_send, all_state_recv.at[lateness], root).start()

        @pl.when(jnp.logical_and(group == 0, jnp.logical_not(is_first)))
        def _():
            target = states.at[seat]
            remote(state, target, mate_state_send, state_recv.at[lateness], mate).start()

    for q, where in enumerate(proxies):

        @pl.when(jnp.logical_and(group == q, jnp.logical_not(is_proxy)))
        def _():
            remote(state, states.at[seat], state_send, state_recv.at[lateness], where).start()

    peak_column = jnp.max(jnp.abs(values), axis=1, keepdims=True)
    peak_row = jnp.max(jnp.where(diagonal, peak_column, 0.0), axis=0, keepdims=True)
    peak_message[...] = jnp.zeros_like(peak_message)
    for line in range(lines):
        low = line * width
        high = min(low + width, blocks)
        peak_message[pl.ds(line, 1), : high - low] = peak_row[:, low:high]

    for where in mates + [collector]:

        @unless(at_place(where))
        def _():
            remote(peak_message, peak_received.at[me], peak_send, peak_recv, where).start()

    for q, where in list(enumerate(proxies))[1:]:
        send_part(q, where)

    def top_of_all():
        peak_received[me] = peak_message[...]
        drain(peak_received.at[pl.ds(0, n - 1)], peak_recv)
        return jnp.max(peak_received[...], axis=0)

    def column_of(values, first, rows):
        at_row = lax.broadcasted_iota(jnp.int32, (rows, blocks), 0)
        at_lane = lax.broadcasted_iota(jnp.int32, (rows, blocks), 1)
        return jnp.sum(jnp.where(at_lane == at_row + first, values, 0.0), axis=1, keepdims=True)

    def run_if(flag, step):
        if isinstance(flag, bool):
            if flag:
                step()
        else:
            pl.when(flag)(step)

    def negated(flag):
        return not flag if isinstance(flag, bool) else jnp.logical_not(flag)

    def place_states(target, source, owners, late):
        for at in range(owners):
            if (at % fsdp == last) == late:
                for kind in range(3):
                    target[kind, pl.ds(at * owned, owned), :] = source[at, kind]

    def summed(inbox, first, rows):
        return jnp.sum(inbox[pl.ds(first, rows)].astype(jnp.float32), axis=0)

    if mates:
        for at, (combiner, near) in enumerate(zip(combiners, nears)):

            @pl.when(at_place(combiner))
            def _():
                own = combiner in near
                if own:
                    near_received[near.index(combiner)] = message[pl.ds(skip, kept), :]
                drain(near_received.at[pl.ds(0, len(near) - own)], near_recv)
                partial_out[...] = summed(near_received, 0, len(near))
                remote(partial_out, partial_in.at[at], partial_send, partial_recv, root).start()

    @pl.when(is_collector)
    def _():
        top = top_of_all()
        peak_out[...] = top

        def spread_top(where):
            remote(peak_out, peak_in, top_send, top_recv, where).start()

        others(spread_top, mates)
        peak_in[...] = top

    if mates:

        @pl.when(is_root)
        def _():
            all_received[slot] = message[pl.ds(skip, kept), :]
            own_scale = column_of(scale, skip, kept)
            owners = kept // owned
            total = None
            for f in range(fsdp):
                direct = dp // 2 if f < near_levels else dp
                if f == last:
                    drain(all_states.at[pl.ds(0, (dp - pair) * last)], all_state_recv.at[0])
                    place_states(all_column, all_states, owners, False)
                    drain(partial_in, partial_recv)
                    total = total + summed(partial_in, 0, half)
                    drain(all_states.at[pl.ds(0, dp - pair)], all_state_recv.at[1])
                    place_states(all_column, all_states, owners, True)
                drain(all_received.at[pl.ds(0, direct - (f == root[1]))], all_recv.at[f])
                more = summed(all_received, f * dp, direct)
                total = more if total is None else total + more
            gradient = total * own_scale
            updated, _, _ = adamw(gradient, all_column[0], all_column[1], all_column[2])
            ready = weights_ref.at[pl.ds(skip, kept)]
            weights_ref[pl.ds(skip, kept), :] = updated.astype(jnp.bfloat16)
            for where in mates[:-1]:
                remote(ready, ready, out_send, out_recv, where).start()

    if mates:

        @pl.when(is_first)
        def _():
            states[pl.ds(seat, 1)] = state[...][None]
            own_scale = column_of(scale, 0, part)
            drain(states.at[pl.ds(0, pair * last - 1)], state_recv.at[0])
            place_states(column, states, pair * fsdp, False)
            drain(states.at[pl.ds(0, pair)], state_recv.at[1])
            place_states(column, states, pair * fsdp, True)
            drain(early_in, early_recv)
            drain(received.at[pl.ds(0, dp)], recv_sems.at[last])
            gradient = (early_in[...] + summed(received, last * dp, dp)) * own_scale
            codes[...] = gradient
            own = (mate[0] * fsdp + mate[1]) * owned
            gradient_in[...] = codes[pl.ds(own, owned), :]
            updated, _, _ = adamw(gradient, column[0], column[1], column[2])
            weights_ref[pl.ds(0, part), :] = updated.astype(jnp.bfloat16)

    def reduce_part(mine, level):
        group = mine // pair if isinstance(mine, int) else lax.div(mine, pair)
        seat = (mine - group * pair) * fsdp + level
        first = group * part
        if not isinstance(first, int):
            first = pl.multiple_of(first, 8)
        received[pl.ds(level * dp + mine, 1)] = message[pl.ds(first, part)][None]
        states[pl.ds(seat, 1)] = state[...][None]
        own_scale = column_of(scale, first, part)
        at_last = proxies[0][1] == last
        total = None
        for f in range(fsdp):
            if f == last:
                if mates and group == 0:
                    early_out[...] = total
                    remote(early_out, early_in, early_send, early_recv, mate).start()
                drain(states.at[pl.ds(0, pair * last - (not at_last))], state_recv.at[0])
                place_states(column, states, pair * fsdp, False)
                drain(states.at[pl.ds(0, pair - at_last)], state_recv.at[1])
                place_states(column, states, pair * fsdp, True)
            own_level = level == f
            run_if(own_level, lambda: drain(received.at[pl.ds(0, dp - 1)], recv_sems.at[f]))
            run_if(negated(own_level), lambda: drain(received.at[pl.ds(0, dp)], recv_sems.at[f]))
            more = summed(received, f * dp, dp)
            total = more if total is None else total + more
        gradient = total * own_scale
        codes[...] = gradient

        def hand_out(at):
            gradient_out[at] = codes[pl.ds(at * owned, owned), :]
            where = (group * pair + at // fsdp, at % fsdp)

            def send():
                remote(gradient_out.at[at], gradient_in, grad_send, grad_recv, where).start()

            run_if(negated(seat == at), send)

        lines_of = pl.ds(first, part)
        ready = weights_ref.at[lines_of]

        def spread(where):
            remote(ready, ready, out_send, out_recv, where).start()

        served = [root] if mates and group == 0 else []
        early = [where[0] * fsdp + where[1] for where in served]
        skipped = [mate[0] * fsdp + mate[1]] if served else []
        late = [at for at in range(pair * fsdp) if at not in early + skipped]
        for at in early if served else late:
            hand_out(at)
        updated, _, _ = adamw(gradient, column[0], column[1], column[2])
        weights_ref[lines_of, :] = updated.astype(jnp.bfloat16)
        for where in served:
            spread(where)
        for at in late if served else early:
            hand_out(at)
        if isinstance(mine, int):
            for where in [(k, f) for k in range(dp) for f in range(fsdp)]:
                if where != (mine, level) and where not in mates:
                    spread(where)
        else:
            others(spread)
        gradient_in[...] = gradient_out[seat]

    if mates:
        for where in proxies:
            pl.when(at_place(where))(functools.partial(reduce_part, *where))
    else:
        pl.when(is_proxy)(functools.partial(reduce_part, mine, level))

    @unless(jnp.logical_or(is_proxy, is_first) if mates else is_proxy)
    def _():
        drain(gradient_in, grad_recv)

    updated, first, second = adamw(gradient_in[...], state[0], state[1], state[2])
    updated_ref[...] = updated
    first_ref[...] = first
    second_ref[...] = second

    @pl.when(is_mate)
    def _():
        peak_in[...] = top_of_all()

    @unless(any_of([is_collector, is_mate]))
    def _():
        drain(peak_in, top_recv)

    for line in range(lines):
        low = line * width
        high = min(low + width, blocks)
        peak_ref[:, low:high] = peak_in[pl.ds(line, 1), : high - low]

    @unless(is_proxy)
    def _():
        drain(message, send_sem)
        drain(state, state_send)

    @pl.when(is_proxy)
    def _():
        drain(message.at[pl.ds(0, (count - 1) * part)], send_sem)

    if mates:

        @unless(jnp.logical_or(is_root, is_idle))
        def _():
            drain(rest, all_send)

        @pl.when(is_kept)
        def _():
            drain(state, all_state_send)

        @pl.when(any_of([at_place(where) for where in combiners]))
        def _():
            drain(partial_out, partial_send)

        @pl.when(at_place(proxies[0]))
        def _():
            drain(early_out, early_send)

        @pl.when(level == last)
        def _():
            drain(message.at[pl.ds(0, part)], far_send)

        @pl.when(jnp.logical_and(group == 0, jnp.logical_not(is_first)))
        def _():
            drain(state, mate_state_send)

    inboxes = len(mates) + 1
    is_inbox = any_of([is_mate, is_collector])

    @pl.when(is_inbox)
    def _():
        if inboxes > 1:
            drain(peak_received.at[pl.ds(0, inboxes - 1)], peak_send)

    @unless(is_inbox)
    def _():
        drain(peak_received.at[pl.ds(0, inboxes)], peak_send)

    @pl.when(is_proxy)
    def _():
        drain(weights_ref.at[pl.ds(0, (count - 1) * part)], out_recv)

    for at, where in enumerate(proxies):

        @pl.when(at_place(where))
        def _():
            unserved = 1 if mates and at == 0 else 0
            drain(gradient_out.at[pl.ds(0, pair * fsdp - 1 - unserved)], grad_send)

    if mates:

        @pl.when(is_root)
        def _():
            drain(weights_ref.at[pl.ds(0, skip)], out_recv)
            for where in mates[:-1]:
                drain(rest, out_send)

        @pl.when(is_first)
        def _():
            drain(rest, out_recv)

        @unless(any_of([is_proxy, is_mate]))
        def _():
            drain(weights_ref, out_recv)

        for at, where in enumerate(proxies):
            reached = n - 1 - (len(mates) if at else 1)

            @pl.when(at_place(where))
            def _():
                drain(received.at[pl.ds(0, reached)], out_send)

    else:

        @unless(is_proxy)
        def _():
            drain(weights_ref, out_recv)

        @pl.when(is_proxy)
        def _():
            drain(received.at[pl.ds(0, n - 1)], out_send)

    @pl.when(is_collector)
    def _():
        drain(peak_received.at[pl.ds(0, n - 1 - len(mates))], top_send)


def finish_kernel(*refs):
    count = (len(refs) - 1) // 2
    sems = refs[-1]
    stores = [
        pltpu.make_async_copy(refs[at], refs[count + at], sems.at[at])
        for at in range(count)
    ]
    for store in stores:
        store.start()
    for store in stores:
        store.wait()


def body(sizes, grads, last_peak, master, moment1, moment2):
    dp, fsdp = sizes
    n = dp * fsdp
    blocks, width = grads.shape[1:]
    pair, proxies, _, mates = layout(sizes, blocks, width)
    count = len(proxies)
    owned = master.shape[0]
    part = blocks // count
    lines = pl.cdiv(blocks, width)
    f32, bf16 = jnp.float32, jnp.bfloat16
    vmem = pl.BlockSpec(memory_space=pltpu.VMEM)
    anywhere = pl.BlockSpec(memory_space=pl.ANY)
    shapes = (
        ((owned, width), f32),
        ((owned, width), f32),
        ((owned, width), f32),
        ((blocks, width), bf16),
        ((1, blocks), f32),
    )
    kept = blocks - part
    near_levels, half, _ = gathering(sizes)
    root_scratch = [
        pltpu.VMEM((n, kept, width), bf16),
        pltpu.VMEM((kept // owned, 3, owned, width), f32),
        pltpu.VMEM((3, kept, width), f32),
        pltpu.VMEM((near_levels * pair, kept, width), bf16),
        pltpu.VMEM((kept, width), f32),
        pltpu.VMEM((half, kept, width), f32),
        pltpu.SemaphoreType.DMA((fsdp,)),
        pltpu.SemaphoreType.DMA,
        pltpu.SemaphoreType.DMA,
        pltpu.SemaphoreType.DMA((2,)),
        pltpu.SemaphoreType.DMA,
        pltpu.SemaphoreType.DMA,
        pltpu.SemaphoreType.DMA,
        pltpu.VMEM((part, width), f32),
        pltpu.VMEM((part, width), f32),
    ] + [pltpu.SemaphoreType.DMA] * 4
    results = pl.pallas_call(
        functools.partial(kernel, sizes),
        out_shape=tuple(pltpu.VMEM(shape, kind) for shape, kind in shapes),
        in_specs=[anywhere] * 5,
        out_specs=(vmem,) * 5,
        scratch_shapes=[
            pltpu.VMEM((1, blocks, width), f32),
            pltpu.VMEM((1, blocks), f32),
            pltpu.VMEM((3, owned, width), f32),
            pltpu.VMEM((part, width), f32),
            pltpu.VMEM((blocks, width), bf16),
            pltpu.VMEM((n, part, width), bf16),
            pltpu.VMEM((pair * fsdp, 3, owned, width), f32),
            pltpu.VMEM((3, part, width), f32),
            pltpu.VMEM((pair * fsdp, owned, width), f32),
            pltpu.VMEM((owned, width), f32),
            pltpu.VMEM((lines, width), f32),
            pltpu.VMEM((n, lines, width), f32),
            pltpu.VMEM((lines, width), f32),
            pltpu.VMEM((lines, width), f32),
            pltpu.SemaphoreType.DMA((6,)),
            pltpu.SemaphoreType.DMA((fsdp,)),
        ]
        + [pltpu.SemaphoreType.DMA] * 2
        + [pltpu.SemaphoreType.DMA((2,))]
        + [pltpu.SemaphoreType.DMA] * 8
        + (root_scratch if mates else []),
        compiler_params=pltpu.CompilerParams(collective_id=0, has_side_effects=True),
    )(grads, last_peak.reshape(1, blocks), master, moment1, moment2)
    updated, first, second, weights, peak = pl.pallas_call(
        finish_kernel,
        out_shape=tuple(jax.ShapeDtypeStruct(shape, kind) for shape, kind in shapes),
        in_specs=[vmem] * 5,
        out_specs=(anywhere,) * 5,
        scratch_shapes=[pltpu.SemaphoreType.DMA((5,))],
    )(*(pltpu.with_memory_space_constraint(result, pltpu.VMEM) for result in results))
    return (updated, first, second, weights, peak.reshape(blocks))


def solution(mesh):
    sharded = P(AXES, None)
    return jax.shard_map(
        functools.partial(body, (mesh.shape["dp"], mesh.shape["fsdp"])),
        mesh=mesh,
        in_specs=(P(AXES, None, None), P(), sharded, sharded, sharded),
        out_specs=(sharded, sharded, sharded, P(), P()),
        check_vma=False,
    )
```

profile of v0, /device:TPU:0, one launch (start us, length us, event | category | flops | bytes accessed | tf_op | source)
XLA Modules:
  0.0 12.2 jit_solution(6552696518593043359)
XLA Ops:
  0.6 10.9 %shard_map.92 = (f32[3,128]{1,0:T(4,128)S(1)}, f32[3,128]{1,0:T(4,128)S(1)}, f32[3,128]{1,0:T(4,128)S(1)}, bf16[96,128]{1,0:T(8,128)(2,1)S(1)}, f32[1,96]{1,0:T(1,128)S(1)}) custom-call(f32[1,96,128]{2,1,0:T(8,128)} %grads_hbm.1, f32[1,96]{1,0:T(1,128)} %bitcast.2, f32[3,128]{1,0:T(4,128)} %master_hbm.1, f32[3,128]{1,0:T(4,128)} %moment1_hbm.1, ...), custom_call_target="tpu_custom_call" | custom-call | tf_op jit(solution)/shard_map/pallas_call | solution.py:686
  11.6 0.7 %shard_map.93 = (f32[3,128]{1,0:T(4,128)}, f32[3,128]{1,0:T(4,128)}, f32[3,128]{1,0:T(4,128)}, bf16[96,128]{1,0:T(8,128)(2,1)}, f32[1,96]{1,0:T(1,128)}) custom-call(f32[3,128]{1,0:T(4,128)S(1)} %get-tuple-element.15.refs_0_, f32[3,128]{1,0:T(4,128)S(1)} %get-tuple-element.16.refs_1_, f32[3,128]{1,0:T(4,128)S(1)} %get-tuple-element.17.refs_2_, ...), custom_call_target="tpu_custom_call" | custom-call | tf_op jit(solution)/shard_map/pallas_call | solution.py:715
where the time goes:
time: 12.4 us; the launch traced here: 12.2 us
  Pallas kernels  11.6 us (94%)
  between operations  0.64 us (5%)
    pallas_call x1, Pallas kernels, body(): pl.pallas_call(functools.partial(kernel, sizes), out_shape=tuple((pltpu.V...  10.9 us
    pallas_call x1, Pallas kernels, body(): pl.pallas_call(finish_kernel, out_shape=tuple((jax.ShapeDtypeStruct(shape...  0.67 us

commit v1 on v0

--- a/solution.py
+++ b/solution.py
@@ -48,9 +48,9 @@
 
 def gathering(sizes):
     dp, fsdp = sizes
-    half = dp // 4
-    places = [(2 * g + 1 if g == half else 2 * (g - half) + 1, 0) for g in range(half, 2 * half)]
-    return min(2, fsdp - 1), half, places
+    chips = dp // 2
+    count = chips // 4
+    return min(2, fsdp - 1), count, [(2 * (g - chips // 2) + 1, 0) for g in range(chips - count, chips)]
 
 
 def kernel(
@@ -130,12 +130,13 @@
         is_kept = me * owned >= skip
         mate = mates[0]
         is_first = at_place(mate)
-        near_levels, half, combiners = gathering(sizes)
+        near_levels, gathered, combiners = gathering(sizes)
+        tops = dp // pair - gathered
         nears = []
-        for at in range(half):
-            chip = (half + at) * pair
+        for at in range(gathered):
+            chip = (tops + at) * pair
             nears.append([(k, f) for f in range(near_levels) for k in range(chip, chip + pair)])
-        in_nears = [jnp.logical_and(level < near_levels, group == half + at) for at in range(half)]
+        in_nears = [jnp.logical_and(level < near_levels, group == tops + at) for at in range(gathered)]
         is_near = any_of(in_nears)
         idle = [where for where, near in zip(combiners, nears) if where in near]
         is_idle = any_of([at_place(where) for where in idle])
@@ -295,6 +296,10 @@
 
     if mates:
 
+        @pl.when(level == last)
+        def _():
+            send_part(0, proxies[0])
+
         @unless(jnp.logical_or(is_root, is_near))
         def _():
             remote(rest, all_received.at[slot], all_send, all_recv.at[level], root).start()
@@ -303,12 +308,8 @@
 
             @pl.when(jnp.logical_and(in_nears[at], jnp.logical_not(at_place(combiner))))
             def _():
-                target = near_received.at[level * pair + mine - (half + at) * pair]
+                target = near_received.at[level * pair + mine - (tops + at) * pair]
                 remote(rest, target, all_send, near_recv, combiner).start()
-
-        @pl.when(level == last)
-        def _():
-            send_part(0, proxies[0])
 
     for load in loads[3:]:
         load.wait()
@@ -408,12 +409,12 @@
             owners = kept // owned
             total = None
             for f in range(fsdp):
-                direct = dp // 2 if f < near_levels else dp
+                direct = tops * pair if f < near_levels else dp
                 if f == last:
                     drain(all_states.at[pl.ds(0, (dp - pair) * last)], all_state_recv.at[0])
                     place_states(all_column, all_states, owners, False)
                     drain(partial_in, partial_recv)
-                    total = total + summed(partial_in, 0, half)
+                    total = total + summed(partial_in, 0, gathered)
                     drain(all_states.at[pl.ds(0, dp - pair)], all_state_recv.at[1])
                     place_states(all_column, all_states, owners, True)
                 drain(all_received.at[pl.ds(0, direct - (f == root[1]))], all_recv.at[f])
@@ -665,14 +666,14 @@
         ((1, blocks), f32),
     )
     kept = blocks - part
-    near_levels, half, _ = gathering(sizes)
+    near_levels, gathered, _ = gathering(sizes)
     root_scratch = [
         pltpu.VMEM((n, kept, width), bf16),
         pltpu.VMEM((kept // owned, 3, owned, width), f32),
         pltpu.VMEM((3, kept, width), f32),
         pltpu.VMEM((near_levels * pair, kept, width), bf16),
         pltpu.VMEM((kept, width), f32),
-        pltpu.VMEM((half, kept, width), f32),
+        pltpu.VMEM((gathered, kept, width), f32),
         pltpu.SemaphoreType.DMA((fsdp,)),
         pltpu.SemaphoreType.DMA,
         pltpu.SemaphoreType.DMA,

time: 12.4 us -> 12.3 us (level)
  the two profiles are of different devices: /device:TPU:0 before, /device:TPU:5 now
where the time goes in v1:
time: 12.3 us; the launch traced here: 12.1 us
  Pallas kernels  11.4 us (93%)
  between operations  0.64 us (5%)
    pallas_call x1, Pallas kernels, body(): pl.pallas_call(functools.partial(kernel, sizes), out_shape=tuple((pltpu.V...  10.8 us
    pallas_call x1, Pallas kernels, body(): pl.pallas_call(finish_kernel, out_shape=tuple((jax.ShapeDtypeStruct(shape...  0.67 us

profile of v1, /device:TPU:5, one launch (start us, length us, event | category | flops | bytes accessed | tf_op | source)
XLA Modules:
  0.0 12.1 jit_solution(12331735370983326479)
XLA Ops:
  0.6 10.8 %shard_map.92 = (f32[3,128]{1,0:T(4,128)S(1)}, f32[3,128]{1,0:T(4,128)S(1)}, f32[3,128]{1,0:T(4,128)S(1)}, bf16[96,128]{1,0:T(8,128)(2,1)S(1)}, f32[1,96]{1,0:T(1,128)S(1)}) custom-call(f32[1,96,128]{2,1,0:T(8,128)} %grads_hbm.1, f32[1,96]{1,0:T(1,128)} %bitcast.2, f32[3,128]{1,0:T(4,128)} %master_hbm.1, f32[3,128]{1,0:T(4,128)} %moment1_hbm.1, ...), custom_call_target="tpu_custom_call" | custom-call | tf_op jit(solution)/shard_map/pallas_call | solution.py:687
  11.4 0.7 %shard_map.93 = (f32[3,128]{1,0:T(4,128)}, f32[3,128]{1,0:T(4,128)}, f32[3,128]{1,0:T(4,128)}, bf16[96,128]{1,0:T(8,128)(2,1)}, f32[1,96]{1,0:T(1,128)}) custom-call(f32[3,128]{1,0:T(4,128)S(1)} %get-tuple-element.15.refs_0_, f32[3,128]{1,0:T(4,128)S(1)} %get-tuple-element.16.refs_1_, f32[3,128]{1,0:T(4,128)S(1)} %get-tuple-element.17.refs_2_, ...), custom_call_target="tpu_custom_call" | custom-call | tf_op jit(solution)/shard_map/pallas_call | solution.py:716

commit v2 on v1

--- a/solution.py
+++ b/solution.py
@@ -51,6 +51,11 @@
     chips = dp // 2
     count = chips // 4
     return min(2, fsdp - 1), count, [(2 * (g - chips // 2) + 1, 0) for g in range(chips - count, chips)]
+
+
+def near_root(sizes):
+    dp, fsdp = sizes
+    return [(3, 0), (dp // 2 + 1, 0)] + [(1, f) for f in range(1, fsdp - 1)]
 
 
 def kernel(
@@ -129,6 +134,7 @@
         rest = message.at[pl.ds(skip, kept)]
         is_kept = me * owned >= skip
         mate = mates[0]
+        beside = near_root(sizes)
         is_first = at_place(mate)
         near_levels, gathered, combiners = gathering(sizes)
         tops = dp // pair - gathered
@@ -424,7 +430,7 @@
             updated, _, _ = adamw(gradient, all_column[0], all_column[1], all_column[2])
             ready = weights_ref.at[pl.ds(skip, kept)]
             weights_ref[pl.ds(skip, kept), :] = updated.astype(jnp.bfloat16)
-            for where in mates[:-1]:
+            for where in [mate] + beside:
                 remote(ready, ready, out_send, out_recv, where).start()
 
     if mates:
@@ -502,8 +508,9 @@
         for at in late if served else early:
             hand_out(at)
         if isinstance(mine, int):
+            unserved = mates if group == 0 else mates + beside
             for where in [(k, f) for k in range(dp) for f in range(fsdp)]:
-                if where != (mine, level) and where not in mates:
+                if where != (mine, level) and where not in unserved:
                     spread(where)
         else:
             others(spread)
@@ -600,8 +607,7 @@
         @pl.when(is_root)
         def _():
             drain(weights_ref.at[pl.ds(0, skip)], out_recv)
-            for where in mates[:-1]:
-                drain(rest, out_send)
+            drain(all_received.at[pl.ds(0, 1 + len(beside))], out_send)
 
         @pl.when(is_first)
         def _():
@@ -612,7 +618,7 @@
             drain(weights_ref, out_recv)
 
         for at, where in enumerate(proxies):
-            reached = n - 1 - (len(mates) if at else 1)
+            reached = n - 1 - (len(mates + beside) if at else 1)
 
             @pl.when(at_place(where))
             def _():

time: 12.3 us -> 12 us (0.976)
  the two profiles are of different devices: /device:TPU:5 before, /device:TPU:0 now
where the time goes in v2:
time: 12 us; the launch traced here: 11.9 us
  Pallas kernels  11.2 us (93%)
  between operations  0.64 us (5%)
    pallas_call x1, Pallas kernels, body(): pl.pallas_call(functools.partial(kernel, sizes), out_shape=tuple((pltpu.V...  10.5 us
    pallas_call x1, Pallas kernels, body(): pl.pallas_call(finish_kernel, out_shape=tuple((jax.ShapeDtypeStruct(shape...  0.67 us

profile of v2, /device:TPU:0, one launch (start us, length us, event | category | flops | bytes accessed | tf_op | source)
XLA Modules:
  0.0 11.9 jit_solution(15839685407016175302)
XLA Ops:
  0.6 10.5 %shard_map.92 = (f32[3,128]{1,0:T(4,128)S(1)}, f32[3,128]{1,0:T(4,128)S(1)}, f32[3,128]{1,0:T(4,128)S(1)}, bf16[96,128]{1,0:T(8,128)(2,1)S(1)}, f32[1,96]{1,0:T(1,128)S(1)}) custom-call(f32[1,96,128]{2,1,0:T(8,128)} %grads_hbm.1, f32[1,96]{1,0:T(1,128)} %bitcast.2, f32[3,128]{1,0:T(4,128)} %master_hbm.1, f32[3,128]{1,0:T(4,128)} %moment1_hbm.1, ...), custom_call_target="tpu_custom_call" | custom-call | tf_op jit(solution)/shard_map/pallas_call | solution.py:693
  11.2 0.7 %shard_map.93 = (f32[3,128]{1,0:T(4,128)}, f32[3,128]{1,0:T(4,128)}, f32[3,128]{1,0:T(4,128)}, bf16[96,128]{1,0:T(8,128)(2,1)}, f32[1,96]{1,0:T(1,128)}) custom-call(f32[3,128]{1,0:T(4,128)S(1)} %get-tuple-element.15.refs_0_, f32[3,128]{1,0:T(4,128)S(1)} %get-tuple-element.16.refs_1_, f32[3,128]{1,0:T(4,128)S(1)} %get-tuple-element.17.refs_2_, ...), custom_call_target="tpu_custom_call" | custom-call | tf_op jit(solution)/shard_map/pallas_call | solution.py:722

commit v3 on v2

--- a/solution.py
+++ b/solution.py
@@ -153,20 +153,10 @@
             near_received,
             partial_out,
             partial_in,
-            all_recv,
-            all_send,
-            all_state_send,
-            all_state_recv,
-            near_recv,
-            partial_send,
-            partial_recv,
             early_out,
             early_in,
-            early_send,
-            early_recv,
-            far_send,
-            mate_state_send,
         ) = root_refs
+        near_recv = recv_sems.at[0]
 
     def remote(source, target, send, recv, where):
         return pltpu.make_async_remote_copy(
@@ -198,7 +188,7 @@
             lax.fori_loop(1, n, turn, 0)
 
     loads = [
-        pltpu.make_async_copy(source, target, in_sems.at[at])
+        pltpu.make_async_copy(source, target, in_sems.at[min(at, 3)])
         for at, (source, target) in enumerate(
             (
                 (last_peak_hbm, last_peak),
@@ -288,7 +278,7 @@
         @pl.when(level == last)
         def _():
             source = message.at[pl.ds(0, part)]
-            remote(source, received.at[slot], far_send, recv_sems.at[level], mate).start()
+            remote(source, received.at[slot], send_sem, recv_sems.at[level], mate).start()
 
         @unless(level == last)
         def _():
@@ -308,28 +298,27 @@
 
         @unless(jnp.logical_or(is_root, is_near))
         def _():
-            remote(rest, all_received.at[slot], all_send, all_recv.at[level], root).start()
+            remote(rest, all_received.at[slot], send_sem, recv_sems.at[level], root).start()
 
         for at, combiner in enumerate(combiners):
 
             @pl.when(jnp.logical_and(in_nears[at], jnp.logical_not(at_place(combiner))))
             def _():
                 target = near_received.at[level * pair + mine - (tops + at) * pair]
-                remote(rest, target, all_send, near_recv, combiner).start()
-
-    for load in loads[3:]:
-        load.wait()
+                remote(rest, target, send_sem, near_recv, combiner).start()
+
+    drain(state, in_sems.at[3])
     if mates:
 
         @pl.when(is_kept)
         def _():
             target = all_states.at[me - skip // owned]
-            remote(state, target, all_state_send, all_state_recv.at[lateness], root).start()
+            remote(state, target, state_send, state_recv.at[lateness], root).start()
 
         @pl.when(jnp.logical_and(group == 0, jnp.logical_not(is_first)))
         def _():
             target = states.at[seat]
-            remote(state, target, mate_state_send, state_recv.at[lateness], mate).start()
+            remote(state, target, state_send, state_recv.at[lateness], mate).start()
 
     for q, where in enumerate(proxies):
 
@@ -393,7 +382,7 @@
                     near_received[near.index(combiner)] = message[pl.ds(skip, kept), :]
                 drain(near_received.at[pl.ds(0, len(near) - own)], near_recv)
                 partial_out[...] = summed(near_received, 0, len(near))
-                remote(partial_out, partial_in.at[at], partial_send, partial_recv, root).start()
+                remote(partial_out, partial_in.at[at], grad_send, top_recv, root).start()
 
     @pl.when(is_collector)
     def _():
@@ -417,13 +406,13 @@
             for f in range(fsdp):
                 direct = tops * pair if f < near_levels else dp
                 if f == last:
-                    drain(all_states.at[pl.ds(0, (dp - pair) * last)], all_state_recv.at[0])
+                    drain(all_states.at[pl.ds(0, (dp - pair) * last)], state_recv.at[0])
                     place_states(all_column, all_states, owners, False)
-                    drain(partial_in, partial_recv)
+                    drain(partial_in, top_recv)
                     total = total + summed(partial_in, 0, gathered)
-                    drain(all_states.at[pl.ds(0, dp - pair)], all_state_recv.at[1])
+                    drain(all_states.at[pl.ds(0, dp - pair)], state_recv.at[1])
                     place_states(all_column, all_states, owners, True)
-                drain(all_received.at[pl.ds(0, direct - (f == root[1]))], all_recv.at[f])
+                drain(all_received.at[pl.ds(0, direct - (f == root[1]))], recv_sems.at[f])
                 more = summed(all_received, f * dp, direct)
                 total = more if total is None else total + more
             gradient = total * own_scale
@@ -443,7 +432,7 @@
             place_states(column, states, pair * fsdp, False)
             drain(states.at[pl.ds(0, pair)], state_recv.at[1])
             place_states(column, states, pair * fsdp, True)
-            drain(early_in, early_recv)
+            drain(early_in, top_recv)
             drain(received.at[pl.ds(0, dp)], recv_sems.at[last])
             gradient = (early_in[...] + summed(received, last * dp, dp)) * own_scale
             codes[...] = gradient
@@ -467,7 +456,7 @@
             if f == last:
                 if mates and group == 0:
                     early_out[...] = total
-                    remote(early_out, early_in, early_send, early_recv, mate).start()
+                    remote(early_out, early_in, top_send, top_recv, mate).start()
                 drain(states.at[pl.ds(0, pair * last - (not at_last))], state_recv.at[0])
                 place_states(column, states, pair * fsdp, False)
                 drain(states.at[pl.ds(0, pair - at_last)], state_recv.at[1])
@@ -544,40 +533,43 @@
         high = min(low + width, blocks)
         peak_ref[:, low:high] = peak_in[pl.ds(line, 1), : high - low]
 
-    @unless(is_proxy)
-    def _():
-        drain(message, send_sem)
-        drain(state, state_send)
-
-    @pl.when(is_proxy)
-    def _():
-        drain(message.at[pl.ds(0, (count - 1) * part)], send_sem)
-
-    if mates:
-
-        @unless(jnp.logical_or(is_root, is_idle))
-        def _():
-            drain(rest, all_send)
-
-        @pl.when(is_kept)
-        def _():
-            drain(state, all_state_send)
+    def tally(flags):
+        return sum(jnp.where(flag, 1, 0) for flag in flags)
+
+    def drain_first(ref, sem, number, most):
+        for value in range(1, most + 1):
+
+            @pl.when(number == value)
+            def _():
+                drain(ref.at[pl.ds(0, value)], sem)
+
+    parts_sent = count - tally([is_proxy])
+    states_sent = tally([jnp.logical_not(is_proxy)])
+    if mates:
+        parts_sent += (count - 1) * tally([jnp.logical_not(jnp.logical_or(is_root, is_idle))])
+        parts_sent += tally([level == last])
+        states_sent += tally([is_kept, jnp.logical_and(group == 0, jnp.logical_not(is_first))])
+        drain_first(received, send_sem, parts_sent, 2 * count)
+        drain_first(states, state_send, states_sent, 3)
 
         @pl.when(any_of([at_place(where) for where in combiners]))
         def _():
-            drain(partial_out, partial_send)
+            drain(partial_out, grad_send)
 
         @pl.when(at_place(proxies[0]))
         def _():
-            drain(early_out, early_send)
-
-        @pl.when(level == last)
-        def _():
-            drain(message.at[pl.ds(0, part)], far_send)
-
-        @pl.when(jnp.logical_and(group == 0, jnp.logical_not(is_first)))
-        def _():
-            drain(state, mate_state_send)
+            drain(early_out, top_send)
+
+    else:
+
+        @unless(is_proxy)
+        def _():
+            drain(message, send_sem)
+            drain(state, state_send)
+
+        @pl.when(is_proxy)
+        def _():
+            drain(message.at[pl.ds(0, (count - 1) * part)], send_sem)
 
     inboxes = len(mates) + 1
     is_inbox = any_of([is_mate, is_collector])
@@ -640,15 +632,16 @@
 
 
 def finish_kernel(*refs):
-    count = (len(refs) - 1) // 2
-    sems = refs[-1]
+    *refs, three, sems = refs
+    count = len(refs) // 2
     stores = [
-        pltpu.make_async_copy(refs[at], refs[count + at], sems.at[at])
+        pltpu.make_async_copy(refs[at], refs[count + at], sems.at[max(at - 2, 0)])
         for at in range(count)
     ]
     for store in stores:
         store.start()
-    for store in stores:
+    pltpu.make_async_copy(three, three, sems.at[0]).wait()
+    for store in stores[3:]:
         store.wait()
 
 
@@ -680,16 +673,9 @@
         pltpu.VMEM((near_levels * pair, kept, width), bf16),
         pltpu.VMEM((kept, width), f32),
         pltpu.VMEM((gathered, kept, width), f32),
-        pltpu.SemaphoreType.DMA((fsdp,)),
-        pltpu.SemaphoreType.DMA,
-        pltpu.SemaphoreType.DMA,
-        pltpu.SemaphoreType.DMA((2,)),
-        pltpu.SemaphoreType.DMA,
-        pltpu.SemaphoreType.DMA,
-        pltpu.SemaphoreType.DMA,
         pltpu.VMEM((part, width), f32),
         pltpu.VMEM((part, width), f32),
-    ] + [pltpu.SemaphoreType.DMA] * 4
+    ]
     results = pl.pallas_call(
         functools.partial(kernel, sizes),
         out_shape=tuple(pltpu.VMEM(shape, kind) for shape, kind in shapes),
@@ -710,7 +696,7 @@
             pltpu.VMEM((n, lines, width), f32),
             pltpu.VMEM((lines, width), f32),
             pltpu.VMEM((lines, width), f32),
-            pltpu.SemaphoreType.DMA((6,)),
+            pltpu.SemaphoreType.DMA((4,)),
             pltpu.SemaphoreType.DMA((fsdp,)),
         ]
         + [pltpu.SemaphoreType.DMA] * 2
@@ -724,7 +710,7 @@
         out_shape=tuple(jax.ShapeDtypeStruct(shape, kind) for shape, kind in shapes),
         in_specs=[vmem] * 5,
         out_specs=(anywhere,) * 5,
-        scratch_shapes=[pltpu.SemaphoreType.DMA((5,))],
+        scratch_shapes=[pltpu.VMEM((3, owned, width), f32), pltpu.SemaphoreType.DMA((3,))],
     )(*(pltpu.with_memory_space_constraint(result, pltpu.VMEM) for result in results))
     return (updated, first, second, weights, peak.reshape(blocks))
 

time: 12 us -> 11.9 us (level)
  Pallas kernels: 11.2 us -> 11 us
    pallas_call x1, Pallas kernels: 10.5 us -> 10.4 us  [body(): pl.pallas_call(functools.partial(kernel, sizes), out_shape=tuple((pltpu.V...]
where the time goes in v3:
time: 11.9 us; the launch traced here: 11.7 us
  Pallas kernels  11 us (92%)
  between operations  0.64 us (5%)
    pallas_call x1, Pallas kernels, body(): pl.pallas_call(functools.partial(kernel, sizes), out_shape=tuple((pltpu.V...  10.4 us
    pallas_call x1, Pallas kernels, body(): pl.pallas_call(finish_kernel, out_shape=tuple((jax.ShapeDtypeStruct(shape...  0.65 us

profile of v3, /device:TPU:0, one launch (start us, length us, event | category | flops | bytes accessed | tf_op | source)
XLA Modules:
  0.0 11.7 jit_solution(3140080499617693234)
XLA Ops:
  0.6 10.4 %shard_map.92 = (f32[3,128]{1,0:T(4,128)S(1)}, f32[3,128]{1,0:T(4,128)S(1)}, f32[3,128]{1,0:T(4,128)S(1)}, bf16[96,128]{1,0:T(8,128)(2,1)S(1)}, f32[1,96]{1,0:T(1,128)S(1)}) custom-call(f32[1,96,128]{2,1,0:T(8,128)} %grads_hbm.1, f32[1,96]{1,0:T(1,128)} %bitcast.2, f32[3,128]{1,0:T(4,128)} %master_hbm.1, f32[3,128]{1,0:T(4,128)} %moment1_hbm.1, ...), custom_call_target="tpu_custom_call" | custom-call | tf_op jit(solution)/shard_map/pallas_call | solution.py:679
  11.0 0.7 %shard_map.93 = (f32[3,128]{1,0:T(4,128)}, f32[3,128]{1,0:T(4,128)}, f32[3,128]{1,0:T(4,128)}, bf16[96,128]{1,0:T(8,128)(2,1)}, f32[1,96]{1,0:T(1,128)}) custom-call(f32[3,128]{1,0:T(4,128)S(1)} %get-tuple-element.15.refs_0_, f32[3,128]{1,0:T(4,128)S(1)} %get-tuple-element.16.refs_1_, f32[3,128]{1,0:T(4,128)S(1)} %get-tuple-element.17.refs_2_, ...), custom_call_target="tpu_custom_call" | custom-call | tf_op jit(solution)/shard_map/pallas_call | solution.py:708

commit v4 on v3

--- a/solution.py
+++ b/solution.py
@@ -91,11 +91,9 @@
     state_recv,
     grad_send,
     grad_recv,
-    out_send,
     out_recv,
     peak_send,
     peak_recv,
-    top_send,
     top_recv,
     *root_refs,
 ):
@@ -156,7 +154,10 @@
             early_out,
             early_in,
         ) = root_refs
+        out_send = send_sem
         near_recv = recv_sems.at[0]
+    else:
+        (out_send,) = root_refs
 
     def remote(source, target, send, recv, where):
         return pltpu.make_async_remote_copy(
@@ -271,14 +272,14 @@
         @unless(at_place(where))
         def _():
             source = message.at[pl.ds(q * part, part)]
-            remote(source, received.at[slot], send_sem, recv_sems.at[level], where).start()
+            remote(source, received.at[slot], send_sem, recv_sems.at[lateness], where).start()
 
     if mates:
 
         @pl.when(level == last)
         def _():
             source = message.at[pl.ds(0, part)]
-            remote(source, received.at[slot], send_sem, recv_sems.at[level], mate).start()
+            remote(source, received.at[slot], send_sem, recv_sems.at[lateness], mate).start()
 
         @unless(level == last)
         def _():
@@ -298,7 +299,7 @@
 
         @unless(jnp.logical_or(is_root, is_near))
         def _():
-            remote(rest, all_received.at[slot], send_sem, recv_sems.at[level], root).start()
+            remote(rest, all_received.at[slot], send_sem, recv_sems.at[lateness], root).start()
 
         for at, combiner in enumerate(combiners):
 
@@ -390,7 +391,7 @@
         peak_out[...] = top
 
         def spread_top(where):
-            remote(peak_out, peak_in, top_send, top_recv, where).start()
+            remote(peak_out, peak_in, peak_send, top_recv, where).start()
 
         others(spread_top, mates)
         peak_in[...] = top
@@ -403,18 +404,19 @@
             own_scale = column_of(scale, skip, kept)
             owners = kept // owned
             total = None
-            for f in range(fsdp):
-                direct = tops * pair if f < near_levels else dp
-                if f == last:
-                    drain(all_states.at[pl.ds(0, (dp - pair) * last)], state_recv.at[0])
-                    place_states(all_column, all_states, owners, False)
-                    drain(partial_in, top_recv)
-                    total = total + summed(partial_in, 0, gathered)
-                    drain(all_states.at[pl.ds(0, dp - pair)], state_recv.at[1])
-                    place_states(all_column, all_states, owners, True)
-                drain(all_received.at[pl.ds(0, direct - (f == root[1]))], recv_sems.at[f])
-                more = summed(all_received, f * dp, direct)
+            direct = [tops * pair if f < near_levels else dp for f in range(fsdp)]
+            drain(all_received.at[pl.ds(0, sum(direct[:last]) - 1)], recv_sems.at[0])
+            for f in range(last):
+                more = summed(all_received, f * dp, direct[f])
                 total = more if total is None else total + more
+            drain(all_states.at[pl.ds(0, (dp - pair) * last)], state_recv.at[0])
+            place_states(all_column, all_states, owners, False)
+            drain(partial_in, top_recv)
+            total = total + summed(partial_in, 0, gathered)
+            drain(all_received.at[pl.ds(0, direct[last])], recv_sems.at[1])
+            total = total + summed(all_received, last * dp, direct[last])
+            drain(all_states.at[pl.ds(0, dp - pair)], state_recv.at[1])
+            place_states(all_column, all_states, owners, True)
             gradient = total * own_scale
             updated, _, _ = adamw(gradient, all_column[0], all_column[1], all_column[2])
             ready = weights_ref.at[pl.ds(skip, kept)]
@@ -433,7 +435,7 @@
             drain(states.at[pl.ds(0, pair)], state_recv.at[1])
             place_states(column, states, pair * fsdp, True)
             drain(early_in, top_recv)
-            drain(received.at[pl.ds(0, dp)], recv_sems.at[last])
+            drain(received.at[pl.ds(0, dp)], recv_sems.at[1])
             gradient = (early_in[...] + summed(received, last * dp, dp)) * own_scale
             codes[...] = gradient
             own = (mate[0] * fsdp + mate[1]) * owned
@@ -456,16 +458,17 @@
             if f == last:
                 if mates and group == 0:
                     early_out[...] = total
-                    remote(early_out, early_in, top_send, top_recv, mate).start()
+                    remote(early_out, early_in, grad_send, top_recv, mate).start()
                 drain(states.at[pl.ds(0, pair * last - (not at_last))], state_recv.at[0])
                 place_states(column, states, pair * fsdp, False)
-                drain(states.at[pl.ds(0, pair - at_last)], state_recv.at[1])
-                place_states(column, states, pair * fsdp, True)
-            own_level = level == f
-            run_if(own_level, lambda: drain(received.at[pl.ds(0, dp - 1)], recv_sems.at[f]))
-            run_if(negated(own_level), lambda: drain(received.at[pl.ds(0, dp)], recv_sems.at[f]))
+            if f == 0 and last:
+                drain(received.at[pl.ds(0, dp * last - (not at_last))], recv_sems.at[0])
+            if f == last:
+                drain(received.at[pl.ds(0, dp - at_last)], recv_sems.at[min(last, 1)])
             more = summed(received, f * dp, dp)
             total = more if total is None else total + more
+        drain(states.at[pl.ds(0, pair - at_last)], state_recv.at[1])
+        place_states(column, states, pair * fsdp, True)
         gradient = total * own_scale
         codes[...] = gradient
 
@@ -549,16 +552,16 @@
         parts_sent += (count - 1) * tally([jnp.logical_not(jnp.logical_or(is_root, is_idle))])
         parts_sent += tally([level == last])
         states_sent += tally([is_kept, jnp.logical_and(group == 0, jnp.logical_not(is_first))])
-        drain_first(received, send_sem, parts_sent, 2 * count)
+
+        @unless(jnp.logical_or(is_proxy, is_root))
+        def _():
+            drain_first(received, send_sem, parts_sent, 2 * count)
+
         drain_first(states, state_send, states_sent, 3)
 
         @pl.when(any_of([at_place(where) for where in combiners]))
         def _():
             drain(partial_out, grad_send)
-
-        @pl.when(at_place(proxies[0]))
-        def _():
-            drain(early_out, top_send)
 
     else:
 
@@ -574,9 +577,14 @@
     inboxes = len(mates) + 1
     is_inbox = any_of([is_mate, is_collector])
 
-    @pl.when(is_inbox)
+    @pl.when(is_collector)
     def _():
-        if inboxes > 1:
+        drain(peak_received.at[pl.ds(0, n - 1)], peak_send)
+
+    if mates:
+
+        @pl.when(is_mate)
+        def _():
             drain(peak_received.at[pl.ds(0, inboxes - 1)], peak_send)
 
     @unless(is_inbox)
@@ -592,14 +600,15 @@
         @pl.when(at_place(where))
         def _():
             unserved = 1 if mates and at == 0 else 0
-            drain(gradient_out.at[pl.ds(0, pair * fsdp - 1 - unserved)], grad_send)
+            sent = 2 * pair * fsdp - 2 if unserved else pair * fsdp - 1
+            drain(gradient_out.at[pl.ds(0, sent)], grad_send)
 
     if mates:
 
         @pl.when(is_root)
         def _():
             drain(weights_ref.at[pl.ds(0, skip)], out_recv)
-            drain(all_received.at[pl.ds(0, 1 + len(beside))], out_send)
+            drain(received.at[pl.ds(0, count + (count - 1) * (1 + len(beside)))], send_sem)
 
         @pl.when(is_first)
         def _():
@@ -614,7 +623,8 @@
 
             @pl.when(at_place(where))
             def _():
-                drain(received.at[pl.ds(0, reached)], out_send)
+                sent = 2 * (count - 1) + (where[1] == last) + reached
+                drain(received.at[pl.ds(0, sent)], send_sem)
 
     else:
 
@@ -625,10 +635,6 @@
         @pl.when(is_proxy)
         def _():
             drain(received.at[pl.ds(0, n - 1)], out_send)
-
-    @pl.when(is_collector)
-    def _():
-        drain(peak_received.at[pl.ds(0, n - 1 - len(mates))], top_send)
 
 
 def finish_kernel(*refs):
@@ -687,22 +693,22 @@
             pltpu.VMEM((3, owned, width), f32),
             pltpu.VMEM((part, width), f32),
             pltpu.VMEM((blocks, width), bf16),
-            pltpu.VMEM((n, part, width), bf16),
+            pltpu.VMEM((2 * n if mates else n, part, width), bf16),
             pltpu.VMEM((pair * fsdp, 3, owned, width), f32),
             pltpu.VMEM((3, part, width), f32),
-            pltpu.VMEM((pair * fsdp, owned, width), f32),
+            pltpu.VMEM((2 * pair * fsdp, owned, width), f32),
             pltpu.VMEM((owned, width), f32),
             pltpu.VMEM((lines, width), f32),
             pltpu.VMEM((n, lines, width), f32),
             pltpu.VMEM((lines, width), f32),
             pltpu.VMEM((lines, width), f32),
             pltpu.SemaphoreType.DMA((4,)),
-            pltpu.SemaphoreType.DMA((fsdp,)),
+            pltpu.SemaphoreType.DMA((2,)),
         ]
         + [pltpu.SemaphoreType.DMA] * 2
         + [pltpu.SemaphoreType.DMA((2,))]
-        + [pltpu.SemaphoreType.DMA] * 8
-        + (root_scratch if mates else []),
+        + [pltpu.SemaphoreType.DMA] * 6
+        + (root_scratch if mates else [pltpu.SemaphoreType.DMA]),
         compiler_params=pltpu.CompilerParams(collective_id=0, has_side_effects=True),
     )(grads, last_peak.reshape(1, blocks), master, moment1, moment2)
     updated, first, second, weights, peak = pl.pallas_call(

time: 11.9 us -> 11.8 us (level)
  no operation moved by 1% of the time
where the time goes in v4:
time: 11.8 us; the launch traced here: 11.6 us
  Pallas kernels  11 us (93%)
  between operations  0.64 us (5%)
    pallas_call x1, Pallas kernels, body(): pl.pallas_call(functools.partial(kernel, sizes), out_shape=tuple((pltpu.V...  10.4 us
    pallas_call x1, Pallas kernels, body(): pl.pallas_call(finish_kernel, out_shape=tuple((jax.ShapeDtypeStruct(shape...  0.65 us

profile of v4, /device:TPU:0, one launch (start us, length us, event | category | flops | bytes accessed | tf_op | source)
XLA Modules:
  0.0 11.6 jit_solution(4957773785847517872)
XLA Ops:
  0.6 10.4 %shard_map.92 = (f32[3,128]{1,0:T(4,128)S(1)}, f32[3,128]{1,0:T(4,128)S(1)}, f32[3,128]{1,0:T(4,128)S(1)}, bf16[96,128]{1,0:T(8,128)(2,1)S(1)}, f32[1,96]{1,0:T(1,128)S(1)}) custom-call(f32[1,96,128]{2,1,0:T(8,128)} %grads_hbm.1, f32[1,96]{1,0:T(1,128)} %bitcast.2, f32[3,128]{1,0:T(4,128)} %master_hbm.1, f32[3,128]{1,0:T(4,128)} %moment1_hbm.1, ...), custom_call_target="tpu_custom_call" | custom-call | tf_op jit(solution)/shard_map/pallas_call | solution.py:685
  11.0 0.7 %shard_map.93 = (f32[3,128]{1,0:T(4,128)}, f32[3,128]{1,0:T(4,128)}, f32[3,128]{1,0:T(4,128)}, bf16[96,128]{1,0:T(8,128)(2,1)}, f32[1,96]{1,0:T(1,128)}) custom-call(f32[3,128]{1,0:T(4,128)S(1)} %get-tuple-element.15.refs_0_, f32[3,128]{1,0:T(4,128)S(1)} %get-tuple-element.16.refs_1_, f32[3,128]{1,0:T(4,128)S(1)} %get-tuple-element.17.refs_2_, ...), custom_call_target="tpu_custom_call" | custom-call | tf_op jit(solution)/shard_map/pallas_call | solution.py:714

commit v5 on v4

--- a/solution.py
+++ b/solution.py
@@ -280,6 +280,7 @@
         def _():
             source = message.at[pl.ds(0, part)]
             remote(source, received.at[slot], send_sem, recv_sems.at[lateness], mate).start()
+            send_part(0, proxies[0])
 
         @unless(level == last)
         def _():
@@ -292,10 +293,6 @@
     values = grads[0]
 
     if mates:
-
-        @pl.when(level == last)
-        def _():
-            send_part(0, proxies[0])
 
         @unless(jnp.logical_or(is_root, is_near))
         def _():
@@ -638,16 +635,16 @@
 
 
 def finish_kernel(*refs):
-    *refs, three, sems = refs
+    *refs, shape, sems = refs
     count = len(refs) // 2
     stores = [
-        pltpu.make_async_copy(refs[at], refs[count + at], sems.at[max(at - 2, 0)])
+        pltpu.make_async_copy(refs[at], refs[count + at], sems.at[max(at - 3, 0)])
         for at in range(count)
     ]
     for store in stores:
         store.start()
-    pltpu.make_async_copy(three, three, sems.at[0]).wait()
-    for store in stores[3:]:
+    pltpu.make_async_copy(shape, shape, sems.at[0]).wait()
+    for store in stores[4:]:
         store.wait()
 
 
@@ -716,7 +713,7 @@
         out_shape=tuple(jax.ShapeDtypeStruct(shape, kind) for shape, kind in shapes),
         in_specs=[vmem] * 5,
         out_specs=(anywhere,) * 5,
-        scratch_shapes=[pltpu.VMEM((3, owned, width), f32), pltpu.SemaphoreType.DMA((3,))],
+        scratch_shapes=[pltpu.VMEM((3 + dp * fsdp // 2, owned, width), f32), pltpu.SemaphoreType.DMA((2,))],
     )(*(pltpu.with_memory_space_constraint(result, pltpu.VMEM) for result in results))
     return (updated, first, second, weights, peak.reshape(blocks))
 

time: 11.8 us -> 11.8 us (level)
  no operation moved by 1% of the time
where the time goes in v5:
time: 11.8 us; the launch traced here: 11.6 us
  Pallas kernels  11 us (93%)
  between operations  0.64 us (5%)
    pallas_call x1, Pallas kernels, body(): pl.pallas_call(functools.partial(kernel, sizes), out_shape=tuple((pltpu.V...  10.4 us
    pallas_call x1, Pallas kernels, body(): pl.pallas_call(finish_kernel, out_shape=tuple((jax.ShapeDtypeStruct(shape...  0.64 us

profile of v5, /device:TPU:0, one launch (start us, length us, event | category | flops | bytes accessed | tf_op | source)
XLA Modules:
  0.0 11.6 jit_solution(3291260423903605271)
XLA Ops:
  0.6 10.4 %shard_map.92 = (f32[3,128]{1,0:T(4,128)S(1)}, f32[3,128]{1,0:T(4,128)S(1)}, f32[3,128]{1,0:T(4,128)S(1)}, bf16[96,128]{1,0:T(8,128)(2,1)S(1)}, f32[1,96]{1,0:T(1,128)S(1)}) custom-call(f32[1,96,128]{2,1,0:T(8,128)} %grads_hbm.1, f32[1,96]{1,0:T(1,128)} %bitcast.2, f32[3,128]{1,0:T(4,128)} %master_hbm.1, f32[3,128]{1,0:T(4,128)} %moment1_hbm.1, ...), custom_call_target="tpu_custom_call" | custom-call | tf_op jit(solution)/shard_map/pallas_call | solution.py:682
  11.0 0.6 %shard_map.93 = (f32[3,128]{1,0:T(4,128)}, f32[3,128]{1,0:T(4,128)}, f32[3,128]{1,0:T(4,128)}, bf16[96,128]{1,0:T(8,128)(2,1)}, f32[1,96]{1,0:T(1,128)}) custom-call(f32[3,128]{1,0:T(4,128)S(1)} %get-tuple-element.15.refs_0_, f32[3,128]{1,0:T(4,128)S(1)} %get-tuple-element.16.refs_1_, f32[3,128]{1,0:T(4,128)S(1)} %get-tuple-element.17.refs_2_, ...), custom_call_target="tpu_custom_call" | custom-call | tf_op jit(solution)/shard_map/pallas_call | solution.py:711

commit v6 on v4

--- a/solution.py
+++ b/solution.py
@@ -280,6 +280,7 @@
         def _():
             source = message.at[pl.ds(0, part)]
             remote(source, received.at[slot], send_sem, recv_sems.at[lateness], mate).start()
+            send_part(0, proxies[0])
 
         @unless(level == last)
         def _():
@@ -292,10 +293,6 @@
     values = grads[0]
 
     if mates:
-
-        @pl.when(level == last)
-        def _():
-            send_part(0, proxies[0])
 
         @unless(jnp.logical_or(is_root, is_near))
         def _():

time: 11.8 us -> 11.8 us (level)
  no operation moved by 1% of the time
where the time goes in v6:
time: 11.8 us; the launch traced here: 11.6 us
  Pallas kernels  11 us (93%)
  between operations  0.64 us (5%)
    pallas_call x1, Pallas kernels, body(): pl.pallas_call(functools.partial(kernel, sizes), out_shape=tuple((pltpu.V...  10.4 us
    pallas_call x1, Pallas kernels, body(): pl.pallas_call(finish_kernel, out_shape=tuple((jax.ShapeDtypeStruct(shape...  0.65 us

profile of v6, /device:TPU:0, one launch (start us, length us, event | category | flops | bytes accessed | tf_op | source)
XLA Modules:
  0.0 11.6 jit_solution(6518547479083815429)
XLA Ops:
  0.6 10.4 %shard_map.92 = (f32[3,128]{1,0:T(4,128)S(1)}, f32[3,128]{1,0:T(4,128)S(1)}, f32[3,128]{1,0:T(4,128)S(1)}, bf16[96,128]{1,0:T(8,128)(2,1)S(1)}, f32[1,96]{1,0:T(1,128)S(1)}) custom-call(f32[1,96,128]{2,1,0:T(8,128)} %grads_hbm.1, f32[1,96]{1,0:T(1,128)} %bitcast.2, f32[3,128]{1,0:T(4,128)} %master_hbm.1, f32[3,128]{1,0:T(4,128)} %moment1_hbm.1, ...), custom_call_target="tpu_custom_call" | custom-call | tf_op jit(solution)/shard_map/pallas_call | solution.py:682
  11.0 0.7 %shard_map.93 = (f32[3,128]{1,0:T(4,128)}, f32[3,128]{1,0:T(4,128)}, f32[3,128]{1,0:T(4,128)}, bf16[96,128]{1,0:T(8,128)(2,1)}, f32[1,96]{1,0:T(1,128)}) custom-call(f32[3,128]{1,0:T(4,128)S(1)} %get-tuple-element.15.refs_0_, f32[3,128]{1,0:T(4,128)S(1)} %get-tuple-element.16.refs_1_, f32[3,128]{1,0:T(4,128)S(1)} %get-tuple-element.17.refs_2_, ...), custom_call_target="tpu_custom_call" | custom-call | tf_op jit(solution)/shard_map/pallas_call | solution.py:711
